TPU v7x, 256 devices: a 8x8x2 block of a 8x8x16 slice. The times are simulated.
256 devices in a mesh: grp: 2 (over z), row: 128 (over y, x, core).
Axes of the slice: x: 8, y: 8, z: 2, core: 2. Of those that a mesh axis runs over, the one named last changes fastest.
The devices are a block of a 8x8x16 slice.
Arguments:
- concentration: float32 [16, 1024, 1024], P('grp', 'row'), parts along dimension 0, may hold values from -0.95 to 1.35
- target_mass: float32 [16], P('grp'), parts along dimension 0, may hold values from 0 to 0.4
- mobility: float32 [16], P('grp'), parts along dimension 0, may hold values from 0.5 to 2
Outputs:
- updated: float32 [16, 1024, 1024], P('grp', 'row'), parts along dimension 0
- residual: float32 [16], P('grp'), parts along dimension 0
There are 2 independent parts, one for each index of `grp`. A program takes and returns all parts, laid end to end along the dimension named above; each array names one. Nothing has to cross between parts.
All inputs are finite; a program needn't handle non-finite values.
Results may differ from a plain program's by a relative error of at most 0.00005.
Values sent between devices are 32-bit elements; how exact they have to be, the bound alone decides.
A program may use at most 64 MiB of HBM per device.

v0:
```python
import math

import jax
import jax.numpy as jnp
from jax import lax
from jax.sharding import Mesh
from jax.sharding import PartitionSpec as P

ROW = ("row_0", "row_1", "row_2")


stiffness = 1.0
time_step = 0.05
stabilizer = 2.0


def by_axis(x, axes):
    for axis in axes:
        x = lax.psum(x, axis)
    return x


def make_tables(length):
    blocks = length // 128
    short_range = jnp.arange(blocks, dtype=jnp.int32)
    long_range = jnp.arange(128, dtype=jnp.int32)
    short_angle = (short_range[:, None] * short_range[None, :] % blocks).astype(jnp.float32) * (
        2.0 * math.pi / blocks
    )
    long_angle = (long_range[:, None] * long_range[None, :] % 128).astype(jnp.float32) * (
        2.0 * math.pi / 128
    )
    twist_angle = (short_range[:, None] * long_range[None, :]).astype(jnp.float32) * (
        2.0 * math.pi / length
    )
    return (
        jnp.cos(short_angle),
        jnp.sin(short_angle),
        jnp.cos(long_angle),
        jnp.sin(long_angle),
        jnp.cos(twist_angle),
        jnp.sin(twist_angle),
    )


def product(pattern, real_part, imag_part, cosine, sine, orient, real_only=False):

    def contract(operand, table):
        return jnp.einsum(pattern, operand, table, precision=lax.Precision.HIGHEST)

    if imag_part is None:
        return (contract(real_part, cosine), orient * contract(real_part, sine))
    if real_only:
        return (contract(real_part, cosine) - orient * contract(imag_part, sine), None)
    return (
        contract(real_part, cosine) - orient * contract(imag_part, sine),
        contract(imag_part, cosine) + orient * contract(real_part, sine),
    )


def rotate(real_part, imag_part, tables, orient):
    cosine, sine = (tables[4], tables[5])
    return (
        real_part * cosine - orient * imag_part * sine,
        imag_part * cosine + orient * real_part * sine,
    )


def forward_rows(real_field, tables, imag_field=None):
    planes, narrow, length = real_field.shape
    block_shape = (planes, narrow, length // 128, 128)
    shaped = real_field.reshape(block_shape)
    imag_shaped = None
    real_part, imag_part = product("pxab,ac->pxcb", shaped, imag_shaped, tables[0], tables[1], -1.0)
    real_part, imag_part = rotate(real_part, imag_part, tables, -1.0)
    real_part, imag_part = product(
        "pxcb,bd->pcdx", real_part, imag_part, tables[2], tables[3], -1.0
    )
    return (real_part.reshape(planes, length, narrow), imag_part.reshape(planes, length, narrow))


def forward_cols(pieces, tables):
    real_part, imag_part = pieces
    planes, narrow, length = real_part.shape
    shape = (planes, narrow, length // 128, 128)
    real_part, imag_part = product(
        "pqab,ac->pqcb",
        real_part.reshape(shape),
        imag_part.reshape(shape),
        tables[0],
        tables[1],
        -1.0,
    )
    real_part, imag_part = rotate(real_part, imag_part, tables, -1.0)
    real_part, imag_part = product(
        "pqcb,bd->pqcd", real_part, imag_part, tables[2], tables[3], -1.0
    )
    return (real_part.reshape(planes, narrow, length), imag_part.reshape(planes, narrow, length))


def inverse_cols(real_part, imag_part, tables):
    planes, narrow, length = real_part.shape
    shape = (planes, narrow, length // 128, 128)
    real_part, imag_part = product(
        "pqcd,db->pqcb",
        real_part.reshape(shape),
        imag_part.reshape(shape),
        tables[2],
        tables[3],
        1.0,
    )
    real_part, imag_part = rotate(real_part, imag_part, tables, 1.0)
    real_part, imag_part = product("pqcb,ca->pabq", real_part, imag_part, tables[0], tables[1], 1.0)
    return (real_part.reshape(planes, length, narrow), imag_part.reshape(planes, length, narrow))


def inverse_rows(pieces, tables):
    real_part, imag_part = pieces
    planes, narrow, length = real_part.shape
    shape = (planes, narrow, length // 128, 128)
    real_part, imag_part = product(
        "pxcd,db->pxcb",
        real_part.reshape(shape),
        imag_part.reshape(shape),
        tables[2],
        tables[3],
        1.0,
    )
    real_part, imag_part = rotate(real_part, imag_part, tables, 1.0)
    real_part, imag_part = product(
        "pxcb,ca->pxab", real_part, imag_part, tables[0], tables[1], 1.0, True
    )
    real_part = real_part.reshape(planes, narrow, length)
    return real_part


def digit_natural(positions, length):
    blocks = length // 128
    return positions // 128 + blocks * (positions % 128)


def wavenumbers(natural_index, length):
    signed = jnp.where(natural_index < length // 2, natural_index, natural_index - length)
    angular = signed.astype(jnp.float32) * (2.0 * math.pi / length)
    return (angular, jnp.where(natural_index == length // 2, jnp.float32(0.0), angular))


def local(concentration, target_mass, mobility):
    planes, rows_local, width_y = concentration.shape
    devices = lax.axis_size(ROW)
    width_x = rows_local * devices
    cols_local = width_y // devices
    cells = float(width_x * width_y)
    inverse_cells = 1.0 / cells
    residual = by_axis(jnp.sum(concentration, axis=(1, 2)), ROW) / cells - target_mass
    tables_y = make_tables(width_y)
    device = lax.axis_index(ROW)
    local_slots = jnp.arange(cols_local, dtype=jnp.int32)
    columns = device * cols_local + local_slots
    all_x = jnp.arange(width_x, dtype=jnp.int32)
    natural_x = digit_natural(all_x, width_x)
    angular_x, slope_x = wavenumbers(natural_x, width_x)
    angular_x, slope_x = (angular_x[None, :], slope_x[None, :])
    cubic_term = concentration * concentration * concentration - concentration

    def to_spectrum(pieces):
        return forward_cols(pieces, tables_y)

    angular_y, slope_y = wavenumbers(digit_natural(columns, width_y), width_y)
    stacked = jnp.concatenate([concentration, cubic_term], axis=0)
    half_real, half_imag = forward_rows(stacked, tables_y)
    spec_real, spec_imag = to_spectrum(
        (
            lax.all_to_all(half_real, ROW, split_axis=1, concat_axis=2, tiled=True),
            lax.all_to_all(half_imag, ROW, split_axis=1, concat_axis=2, tiled=True),
        )
    )
    field_real, field_imag = (spec_real[:planes], spec_imag[:planes])
    cubic_real, cubic_imag = (spec_real[planes:], spec_imag[planes:])
    angular_y, slope_y = (angular_y[:, None], slope_y[:, None])
    square = angular_x * angular_x + angular_y * angular_y
    chem_real = (cubic_real + stiffness * square * field_real) * inverse_cells
    chem_imag = (cubic_imag + stiffness * square * field_imag) * inverse_cells
    stack_real = jnp.concatenate([-slope_x * chem_imag, -slope_y * chem_imag], axis=0)
    stack_imag = jnp.concatenate([slope_x * chem_real, slope_y * chem_real], axis=0)
    back_real, back_imag = inverse_cols(stack_real, stack_imag, tables_y)
    gradient_pair = inverse_rows(
        (
            lax.all_to_all(back_real, ROW, split_axis=1, concat_axis=2, tiled=True),
            lax.all_to_all(back_imag, ROW, split_axis=1, concat_axis=2, tiled=True),
        ),
        tables_y,
    )
    grad_x = gradient_pair[:planes]
    grad_y = gradient_pair[planes:]
    weight = mobility[:, None, None] / (1.0 + concentration * concentration)
    fluxes = jnp.concatenate([weight * grad_x, weight * grad_y], axis=0)
    flux_half_real, flux_half_imag = forward_rows(fluxes, tables_y)
    flux_real, flux_imag = to_spectrum(
        (
            lax.all_to_all(flux_half_real, ROW, split_axis=1, concat_axis=2, tiled=True),
            lax.all_to_all(flux_half_imag, ROW, split_axis=1, concat_axis=2, tiled=True),
        )
    )
    flux_x_real, flux_x_imag = (flux_real[:planes], flux_imag[:planes])
    flux_y_real, flux_y_imag = (flux_real[planes:], flux_imag[planes:])
    div_real = -slope_x * flux_x_imag - slope_y * flux_y_imag
    div_imag = slope_x * flux_x_real + slope_y * flux_y_real
    factor = (
        time_step
        * inverse_cells
        / (
            1.0
            + time_step
            * mobility[:, None, None]
            * (stabilizer * square + stiffness * square * square)
        )
    )
    change_real, change_imag = inverse_cols(div_real * factor, div_imag * factor, tables_y)
    change = inverse_rows(
        (
            lax.all_to_all(change_real, ROW, split_axis=1, concat_axis=2, tiled=True),
            lax.all_to_all(change_imag, ROW, split_axis=1, concat_axis=2, tiled=True),
        ),
        tables_y,
    )
    fresh = concentration + change
    return (fresh - residual[:, None, None], residual)


def solution(mesh):
    torus = Mesh(
        mesh.devices.reshape(mesh.shape["grp"], 8, 8, 2), ("grp", "row_0", "row_1", "row_2")
    )
    in_specs = (P("grp", ROW, None), P("grp"), P("grp"))
    out_specs = (P("grp", ROW, None), P("grp"))
    return jax.shard_map(local, mesh=torus, in_specs=in_specs, out_specs=out_specs, check_vma=False)
```

profile of v0, /device:TPU:513, one launch (start us, length us, event | category | flops | bytes accessed | tf_op | source)
XLA Modules:
  0.0 410.4 jit_solution(5268577525299020385)
XLA Ops:
  6.6 2.7 copy.114
  9.3 4.2 %reshape.381 = f32[128,1,1024]{2,1,0:T(1,128)} reshape(f32[1024,8,16]{2,1,0:T(8,128)} %bitcast.296) | data formatting | bytes 1048576
  13.5 28.1 %all-to-all-start.1 = ((f32[128,1,1024]{2,1,0:T(1,128)}), f32[128,1,1024]{2,1,0:T(1,128)S(1)}, u32[]{:S(2)}, u32[]{:S(2)}) async-start(f32[128,1,1024]{2,1,0:T(1,128)} %reshape.381), calls=%async_computation.1 | async-start | bytes 1048576 | tf_op jit(solution)/shard_map/all_to_all | solution.py:174
  43.9 2.7 copy.108
  46.6 4.2 %reshape.383 = f32[128,1,1024]{2,1,0:T(1,128)} reshape(f32[1024,8,16]{2,1,0:T(8,128)} %bitcast.297) | data formatting | bytes 1048576
  50.8 10.3 %all-to-all-done.1 = f32[128,1,1024]{2,1,0:T(1,128)S(1)} async-done(((f32[128,1,1024]{2,1,0:T(1,128)}), f32[128,1,1024]{2,1,0:T(1,128)S(1)}, u32[]{:S(2)}, u32[]{:S(2)}) %all-to-all-start.1) | async-done | bytes 524320 | tf_op jit(solution)/shard_map/all_to_all | solution.py:174
  61.0 7.5 %all-to-all-start = ((f32[128,1,1024]{2,1,0:T(1,128)}), f32[128,1,1024]{2,1,0:T(1,128)S(1)}, u32[]{:S(2)}, u32[]{:S(2)}) async-start(f32[128,1,1024]{2,1,0:T(1,128)} %reshape.383), calls=%async_computation | async-start | bytes 1048576 | tf_op jit(solution)/shard_map/all_to_all | solution.py:175
  71.1 2.8 reshape.382
  73.9 4.4 %copy.115 = f32[16,8,128,8]{0,3,2,1:T(8,128)} copy(f32[16,8,128,8]{0,3,1,2:T(8,128)} %bitcast.302) | data formatting | bytes 1048576 | tf_op jit(solution)/shard_map/all_to_all | solution.py:174
  78.3 2.9 copy.116
  81.8 6.3 %all-to-all-done = f32[128,1,1024]{2,1,0:T(1,128)S(1)} async-done(((f32[128,1,1024]{2,1,0:T(1,128)}), f32[128,1,1024]{2,1,0:T(1,128)S(1)}, u32[]{:S(2)}, u32[]{:S(2)}) %all-to-all-start) | async-done | bytes 524320 | tf_op jit(solution)/shard_map/all_to_all | solution.py:175
  88.1 1.9 reduce
  90.0 2.8 reshape.384
  92.7 4.4 %copy.109 = f32[16,8,128,8]{0,3,2,1:T(8,128)} copy(f32[16,8,128,8]{0,3,1,2:T(8,128)} %bitcast.304) | data formatting | bytes 1048576 | tf_op jit(solution)/shard_map/all_to_all | solution.py:175
  97.2 3.3 copy.110
  110.4 3.1 copy.159
  113.5 4.2 %reshape.387 = f32[128,1,1024]{2,1,0:T(1,128)} reshape(f32[1024,8,16]{2,1,0:T(8,128)} %bitcast.298) | data formatting | bytes 1048576
  117.7 10.1 %all-to-all-start.2 = ((f32[128,1,1024]{2,1,0:T(1,128)}), f32[128,1,1024]{2,1,0:T(1,128)S(1)}, u32[]{:S(2)}, u32[]{:S(2)}) async-start(f32[128,1,1024]{2,1,0:T(1,128)} %reshape.387), calls=%async_computation.2 | async-start | bytes 1048576 | tf_op jit(solution)/shard_map/all_to_all | solution.py:189
  129.0 3.1 copy.160
  132.1 4.2 %reshape.385 = f32[128,1,1024]{2,1,0:T(1,128)} reshape(f32[1024,8,16]{2,1,0:T(8,128)} %bitcast.299) | data formatting | bytes 1048576
  136.3 11.1 %all-to-all-done.2 = f32[128,1,1024]{2,1,0:T(1,128)S(1)} async-done(((f32[128,1,1024]{2,1,0:T(1,128)}), f32[128,1,1024]{2,1,0:T(1,128)S(1)}, u32[]{:S(2)}, u32[]{:S(2)}) %all-to-all-start.2) | async-done | bytes 524320 | tf_op jit(solution)/shard_map/all_to_all | solution.py:189
  147.4 7.5 %all-to-all-start.3 = ((f32[128,1,1024]{2,1,0:T(1,128)}), f32[128,1,1024]{2,1,0:T(1,128)S(1)}, u32[]{:S(2)}, u32[]{:S(2)}) async-start(f32[128,1,1024]{2,1,0:T(1,128)} %reshape.385), calls=%async_computation.3 | async-start | bytes 1048576 | tf_op jit(solution)/shard_map/all_to_all | solution.py:190
  154.9 1.9 reduce.3
  156.8 2.9 reshape.388
  159.8 2.5 copy.120
  162.2 6.7 %fusion.104 = f32[16,8,8,128]{3,0,2,1:T(8,128)S(1)} fusion(f32[16,8,8,128]{0,3,2,1:T(8,128)S(1)} %bitcast.292), kind=kOutput, calls=%fused_computation.167 | convolution fusion | flops 201555968 | bytes 1048576 | tf_op jit(solution)/shard_map/pxcd,db->pxcb/dot_general | solution.py:49
  168.9 6.7 %fusion.128 = f32[16,8,8,128]{3,0,2,1:T(8,128)S(1)} fusion(f32[16,8,8,128]{0,3,2,1:T(8,128)S(1)} %bitcast.293), kind=kOutput, calls=%fused_computation.191 | convolution fusion | flops 201555968 | bytes 1048576 | tf_op jit(solution)/shard_map/pxcd,db->pxcb/dot_general | solution.py:49
  175.6 1.9 reduce.2
  177.5 3.1 reshape.386
  180.7 2.5 copy.123
  183.1 6.7 %fusion.106 = f32[16,8,8,128]{3,0,2,1:T(8,128)S(1)} fusion(f32[16,8,8,128]{0,3,2,1:T(8,128)S(1)} %bitcast.294), kind=kOutput, calls=%fused_computation.169 | convolution fusion | flops 201555968 | bytes 1048576 | tf_op jit(solution)/shard_map/pxcd,db->pxcb/dot_general | solution.py:49
  189.8 6.7 %fusion.126 = f32[16,8,8,128]{3,0,2,1:T(8,128)S(1)} fusion(f32[16,8,8,128]{0,3,2,1:T(8,128)S(1)} %bitcast.295), kind=kOutput, calls=%fused_computation.189 | convolution fusion | flops 201555968 | bytes 1048576 | tf_op jit(solution)/shard_map/pxcd,db->pxcb/dot_general | solution.py:49
  203.8 2.7 copy.140
  206.5 4.2 %reshape.389 = f32[128,1,1024]{2,1,0:T(1,128)} reshape(f32[1024,8,16]{2,1,0:T(8,128)} %bitcast.300) | data formatting | bytes 1048576
  210.7 17.1 %all-to-all-start.5 = ((f32[128,1,1024]{2,1,0:T(1,128)}), f32[128,1,1024]{2,1,0:T(1,128)S(1)}, u32[]{:S(2)}, u32[]{:S(2)}) async-start(f32[128,1,1024]{2,1,0:T(1,128)} %reshape.389), calls=%async_computation.5 | async-start | bytes 1048576 | tf_op jit(solution)/shard_map/all_to_all | solution.py:201
  230.1 2.7 copy.134
  232.9 4.2 %reshape.391 = f32[128,1,1024]{2,1,0:T(1,128)} reshape(f32[1024,8,16]{2,1,0:T(8,128)} %bitcast.301) | data formatting | bytes 1048576
  237.0 9.9 %all-to-all-done.5 = f32[128,1,1024]{2,1,0:T(1,128)S(1)} async-done(((f32[128,1,1024]{2,1,0:T(1,128)}), f32[128,1,1024]{2,1,0:T(1,128)S(1)}, u32[]{:S(2)}, u32[]{:S(2)}) %all-to-all-start.5) | async-done | bytes 524320 | tf_op jit(solution)/shard_map/all_to_all | solution.py:201
  247.0 7.5 %all-to-all-start.4 = ((f32[128,1,1024]{2,1,0:T(1,128)}), f32[128,1,1024]{2,1,0:T(1,128)S(1)}, u32[]{:S(2)}, u32[]{:S(2)}) async-start(f32[128,1,1024]{2,1,0:T(1,128)} %reshape.391), calls=%async_computation.4 | async-start | bytes 1048576 | tf_op jit(solution)/shard_map/all_to_all | solution.py:202
  254.5 1.9 reduce.5
  256.4 2.8 reshape.390
  259.1 4.4 %copy.141 = f32[16,8,128,8]{0,3,2,1:T(8,128)} copy(f32[16,8,128,8]{0,3,1,2:T(8,128)} %bitcast.308) | data formatting | bytes 1048576 | tf_op jit(solution)/shard_map/all_to_all | solution.py:201
  263.6 2.9 copy.142
  267.0 7.0 %all-to-all-done.4 = f32[128,1,1024]{2,1,0:T(1,128)S(1)} async-done(((f32[128,1,1024]{2,1,0:T(1,128)}), f32[128,1,1024]{2,1,0:T(1,128)S(1)}, u32[]{:S(2)}, u32[]{:S(2)}) %all-to-all-start.4) | async-done | bytes 524320 | tf_op jit(solution)/shard_map/all_to_all | solution.py:202
  274.0 1.9 reduce.4
  275.9 2.8 reshape.392
  278.7 4.4 %copy.135 = f32[16,8,128,8]{0,3,2,1:T(8,128)} copy(f32[16,8,128,8]{0,3,1,2:T(8,128)} %bitcast.310) | data formatting | bytes 1048576 | tf_op jit(solution)/shard_map/all_to_all | solution.py:202
  283.1 3.0 copy.136
  294.8 3.1 copy.161
  297.9 4.5 %reshape.395 = f32[128,1,512]{2,1,0:T(1,128)} reshape(f32[1024,8,8]{2,1,0:T(8,128)} %bitcast.312) | data formatting | bytes 524288
  302.4 9.3 %all-to-all-start.6 = ((f32[128,1,512]{2,1,0:T(1,128)}), f32[128,1,512]{2,1,0:T(1,128)S(1)}, u32[]{:S(2)}, u32[]{:S(2)}) async-start(f32[128,1,512]{2,1,0:T(1,128)} %reshape.395), calls=%async_computation.6 | async-start | bytes 524288 | tf_op jit(solution)/shard_map/all_to_all | solution.py:222
  312.5 3.1 copy.164
  315.6 4.5 %reshape.393 = f32[128,1,512]{2,1,0:T(1,128)} reshape(f32[1024,8,8]{2,1,0:T(8,128)} %bitcast.313) | data formatting | bytes 524288
  320.1 5.9 %all-to-all-done.6 = f32[128,1,512]{2,1,0:T(1,128)S(1)} async-done(((f32[128,1,512]{2,1,0:T(1,128)}), f32[128,1,512]{2,1,0:T(1,128)S(1)}, u32[]{:S(2)}, u32[]{:S(2)}) %all-to-all-start.6) | async-done | bytes 262176 | tf_op jit(solution)/shard_map/all_to_all | solution.py:222
  326.0 10.4 %all-to-all-start.7 = ((f32[128,1,512]{2,1,0:T(1,128)}), f32[128,1,512]{2,1,0:T(1,128)S(1)}, u32[]{:S(2)}, u32[]{:S(2)}) async-start(f32[128,1,512]{2,1,0:T(1,128)} %reshape.393), calls=%async_computation.7 | async-start | bytes 524288 | tf_op jit(solution)/shard_map/all_to_all | solution.py:223
  336.4 16.2 %psum.21 = f32[8]{0:T(128)S(1)} all-reduce(f32[8]{0:T(128)S(1)} %get-tuple-element.14), channel_id=1, replica_groups=mesh['grp'=2,'row_0'=8,'row_1'=8,'row_2'=2] {'row_0'}, use_global_device_ids=true, to_apply=%region_1.0 | all-reduce | flops 8 | bytes 64 | tf_op jit(solution)/shard_map/psum | solution.py:19
  352.6 12.9 %psum.22 = f32[8]{0:T(128)S(1)} all-reduce(f32[8]{0:T(128)S(1)} %psum.21), channel_id=1, replica_groups=mesh['grp'=2,'row_0'=8,'row_1'=8,'row_2'=2] {'row_1'}, use_global_device_ids=true, to_apply=%region_2.0 | all-reduce | flops 8 | bytes 64 | tf_op jit(solution)/shard_map/psum | solution.py:19
  365.5 9.7 %psum.23 = f32[8]{0:T(128)S(1)} all-reduce(f32[8]{0:T(128)S(1)} %psum.22), channel_id=1, replica_groups=mesh['grp'=2,'row_0'=8,'row_1'=8,'row_2'=2] {'row_2'}, use_global_device_ids=true, to_apply=%region_3.0 | all-reduce | flops 8 | bytes 64 | tf_op jit(solution)/shard_map/psum | solution.py:19
  376.5 3.6 reshape.396
  380.1 6.6 %copy.147 = f32[8,8,128,8]{3,2,1,0:T(8,128)} copy(f32[8,8,128,8]{3,0,1,2:T(8,128)} %bitcast.314) | data formatting | bytes 524288 | tf_op jit(solution)/shard_map/all_to_all | solution.py:222
  386.7 3.6 reshape.373
  392.2 3.6 reshape.394
  395.8 6.6 %copy.150 = f32[8,8,128,8]{3,2,1,0:T(8,128)} copy(f32[8,8,128,8]{3,0,1,2:T(8,128)} %bitcast.315) | data formatting | bytes 524288 | tf_op jit(solution)/shard_map/all_to_all | solution.py:223
  402.4 3.9 reshape.375
  (91 shorter events, 48.6 us)
Async XLA Ops:
  13.5 47.6 %all-to-all-start.1 = ((f32[128,1,1024]{2,1,0:T(1,128)}), f32[128,1,1024]{2,1,0:T(1,128)S(1)}, u32[]{:S(2)}, u32[]{:S(2)}) async-start(f32[128,1,1024]{2,1,0:T(1,128)} %reshape.381), calls=%async_computation.1 | async-start | bytes 1048576 | tf_op jit(solution)/shard_map/all_to_all | solution.py:174
  61.0 27.1 %all-to-all-start = ((f32[128,1,1024]{2,1,0:T(1,128)}), f32[128,1,1024]{2,1,0:T(1,128)S(1)}, u32[]{:S(2)}, u32[]{:S(2)}) async-start(f32[128,1,1024]{2,1,0:T(1,128)} %reshape.383), calls=%async_computation | async-start | bytes 1048576 | tf_op jit(solution)/shard_map/all_to_all | solution.py:175
  117.7 29.7 %all-to-all-start.2 = ((f32[128,1,1024]{2,1,0:T(1,128)}), f32[128,1,1024]{2,1,0:T(1,128)S(1)}, u32[]{:S(2)}, u32[]{:S(2)}) async-start(f32[128,1,1024]{2,1,0:T(1,128)} %reshape.387), calls=%async_computation.2 | async-start | bytes 1048576 | tf_op jit(solution)/shard_map/all_to_all | solution.py:189
  147.4 28.2 %all-to-all-start.3 = ((f32[128,1,1024]{2,1,0:T(1,128)}), f32[128,1,1024]{2,1,0:T(1,128)S(1)}, u32[]{:S(2)}, u32[]{:S(2)}) async-start(f32[128,1,1024]{2,1,0:T(1,128)} %reshape.385), calls=%async_computation.3 | async-start | bytes 1048576 | tf_op jit(solution)/shard_map/all_to_all | solution.py:190
  196.5 3.4 copy-start
  196.5 3.4 copy-start.1
  210.7 36.3 %all-to-all-start.5 = ((f32[128,1,1024]{2,1,0:T(1,128)}), f32[128,1,1024]{2,1,0:T(1,128)S(1)}, u32[]{:S(2)}, u32[]{:S(2)}) async-start(f32[128,1,1024]{2,1,0:T(1,128)} %reshape.389), calls=%async_computation.5 | async-start | bytes 1048576 | tf_op jit(solution)/shard_map/all_to_all | solution.py:201
  247.0 27.1 %all-to-all-start.4 = ((f32[128,1,1024]{2,1,0:T(1,128)}), f32[128,1,1024]{2,1,0:T(1,128)S(1)}, u32[]{:S(2)}, u32[]{:S(2)}) async-start(f32[128,1,1024]{2,1,0:T(1,128)} %reshape.391), calls=%async_computation.4 | async-start | bytes 1048576 | tf_op jit(solution)/shard_map/all_to_all | solution.py:202
  302.4 23.6 %all-to-all-start.6 = ((f32[128,1,512]{2,1,0:T(1,128)}), f32[128,1,512]{2,1,0:T(1,128)S(1)}, u32[]{:S(2)}, u32[]{:S(2)}) async-start(f32[128,1,512]{2,1,0:T(1,128)} %reshape.395), calls=%async_computation.6 | async-start | bytes 524288 | tf_op jit(solution)/shard_map/all_to_all | solution.py:222
  312.5 62.7 %copy-start.3 = (f32[8]{0:T(128)S(1)}, f32[8]{0:T(128)}, u32[]{:S(2)}) copy-start(f32[8]{0:T(128)} %param.4) | copy-start | bytes 100
  326.0 64.9 %all-to-all-start.7 = ((f32[128,1,512]{2,1,0:T(1,128)}), f32[128,1,512]{2,1,0:T(1,128)S(1)}, u32[]{:S(2)}, u32[]{:S(2)}) async-start(f32[128,1,512]{2,1,0:T(1,128)} %reshape.393), calls=%async_computation.7 | async-start | bytes 524288 | tf_op jit(solution)/shard_map/all_to_all | solution.py:223
  375.2 33.9 %copy-start.2 = (f32[8]{0:T(128)}, f32[8]{0:T(128)S(1)}, u32[]{:S(2)}) copy-start(f32[8]{0:T(128)S(1)} %multiply_subtract_fusion.13) | copy-start | bytes 100
where the time goes:
time: 418 us; the launch traced here: 410 us
  local copies, waits for them, and re-layouts  139 us (33%)
  starting transfers between devices  97.4 us (23%)
  matrix products  65.4 us (16%)
  waiting for transfers between devices  50.5 us (12%)
  blocking collectives  38.8 us (9%)
  other arithmetic  17.4 us (4%)
    dot_general x56, matrix products, contract(): return jnp.einsum(pattern, operand, table, precision=lax.Precision.HIGHEST)  65.4 us
    unnamed x24, local copies, waits for them, and re-layouts  58.3 us
    psum x3, blocking collectives, by_axis(): x = lax.psum(x, axis)  38.8 us
    all_to_all x1, starting transfers between devices, local(): lax.all_to_all(half_real, ROW, split_axis=1, concat_axis=2, tiled=True)  28.1 us
    all_to_all x1, starting transfers between devices, local(): lax.all_to_all(flux_half_real, ROW, split_axis=1, concat_axis=2, tiled=True)  17.1 us
    all_to_all x1, waiting for transfers between devices, local(): lax.all_to_all(back_real, ROW, split_axis=1, concat_axis=2, tiled=True)  11.1 us
    all_to_all x1, starting transfers between devices, local(): lax.all_to_all(change_imag, ROW, split_axis=1, concat_axis=2, tiled=True)  10.4 us
    all_to_all x1, waiting for transfers between devices, local(): lax.all_to_all(half_real, ROW, split_axis=1, concat_axis=2, tiled=True)  10.3 us
  transfers between devices with their start and end apart: 8, of which 6 were waited for; matrix products, arithmetic and copies ran while one was open for 24% of the time, Pallas kernels for 0%

commit v1 on v0

v1 whole, which is shorter than its diff:
```python
import functools
import math

import jax
import jax.numpy as jnp
import ml_dtypes
import numpy as np
from jax import lax
from jax.experimental import pallas as pl
from jax.experimental.pallas import tpu as pltpu
from jax.sharding import Mesh
from jax.sharding import PartitionSpec as P

ROW = ("row_0", "row_1", "row_2")
MESH = pl.DeviceIdType.MESH
SIDE = (8, 8, 2)
PEERS = SIDE[0] * SIDE[1] * SIDE[2]
LANES = 128
CHUNKS = 1

stiffness = 1.0
time_step = 0.05
stabilizer = 2.0


def split(table):
    high = table.astype(ml_dtypes.bfloat16)
    low = (table - high.astype(np.float64)).astype(ml_dtypes.bfloat16)
    return np.stack([high, low])


def circulants(length):
    position = np.arange(length)
    signed = np.where(position < length // 2, position, position - length)
    angular = signed * (2.0 * math.pi / length)
    derivative = np.where(position == length // 2, 0.0, angular)
    offset = (position[None, :] - position[:, None]) % length
    second = np.fft.ifft(angular**2).real[offset]
    first = np.fft.ifft(1j * derivative).real[offset]
    return second, first


def real_basis(length):
    wave, is_sine = slots(np.arange(length), length)
    angle = np.outer(np.arange(length), wave) % length * (2.0 * math.pi / length)
    plain = (wave == 0) | (wave == length // 2)
    scale = np.where(plain, np.sqrt(1.0 / length), np.sqrt(2.0 / length))
    return np.where(is_sine & ~plain, np.sin(angle), np.cos(angle)) * scale


def slots(slot, length):
    quarter = length // 4
    odd = slot // (2 * quarter)
    within = slot % (2 * quarter)
    is_sine = within // quarter
    wave = 2 * (within % quarter) + odd
    nyquist = (is_sine == 1) & (wave == 0)
    if isinstance(slot, np.ndarray):
        return np.where(nyquist, length // 2, wave), is_sine == 1
    return jnp.where(nyquist, length // 2, wave), is_sine == 1


def row_tiles(matrix):
    return np.stack([matrix[:256, d * 256 : (d + 1) * 256] for d in range(matrix.shape[0] // 256)])


def column_tiles(matrix, order):
    permuted = matrix[order][:, order]
    blocks = permuted.shape[0] // 256
    out = []
    for d in range(1 - blocks, blocks):
        i, j = max(0, -d), max(0, d)
        out.append(permuted[i * 256 : (i + 1) * 256, j * 256 : (j + 1) * 256])
    return np.stack(out)


@functools.cache
def tables(length, rows_local):
    second, first = circulants(length)
    basis = real_basis(length)
    half = length // 2
    order = np.arange(length).reshape(length // rows_local, rows_local).T.reshape(-1)
    halves = np.stack([basis[:half, :half], basis[:half, half:]])
    back = np.swapaxes(halves, 1, 2)
    return tuple(
        split(t)
        for t in (
            row_tiles(second),
            column_tiles(second, order),
            column_tiles(first, order),
            row_tiles(first),
            halves,
            basis[order],
            basis[order].T,
            back,
        )
    )


def parts(x):
    high = x.astype(jnp.bfloat16)
    low = (x - high.astype(jnp.float32)).astype(jnp.bfloat16)
    return high, jnp.concatenate([high, low], axis=0)


def product(x, pieces):
    m = x.shape[0]
    high, both = parts(x)
    inputs, outputs, piece = pieces
    out = []
    for j in range(outputs):
        total = None
        for i in range(inputs):
            at = slice(i * 256, (i + 1) * 256)
            wide = jnp.dot(both[:, at], piece(i, j, 0), preferred_element_type=jnp.float32)
            narrow = jnp.dot(high[:, at], piece(i, j, 1), preferred_element_type=jnp.float32)
            term = (wide, narrow)
            total = term if total is None else (total[0] + wide, total[1] + narrow)
        out.append(total[0][:m] + total[0][m:] + total[1])
    return jnp.concatenate(out, axis=1)


def by_row(ref):
    n = ref.shape[1]
    return n, n, lambda i, j, part: ref[part, (j - i) % n]


def by_column(ref):
    n = (ref.shape[1] + 1) // 2
    return n, n, lambda i, j, part: ref[part, j - i + n - 1]


def dense(ref):
    n = ref.shape[1] // 256
    return n, n, lambda i, j, part: ref[part, i * 256 : (i + 1) * 256, j * 256 : (j + 1) * 256]


def dense_half(ref, which):
    n = ref.shape[2] // 256
    return n, n, lambda i, j, part: ref[part, which, i * 256 : (i + 1) * 256, j * 256 : (j + 1) * 256]


def kernel(
    x_ref, target_ref, mobility_ref,
    t0, t1, t2, t3, t4, t5, t6, t7,
    out_ref, residual_ref,
    v0, v1, v2, v3, v4, v5, v6, v7,
    send1, take1, send2, take2, send3, take3, send4, take4,
    turn, held, sum_mine, sum_row, sum_total, sum_all,
    table_sem, send_sem, take_sem, sum_send, sum_take,
):
    planes, rows_local, width = x_ref.shape
    ncs = CHUNKS
    each = planes // ncs
    hbm_tables = (t0, t1, t2, t3, t4, t5, t6, t7)
    vmem_tables = (v0, v1, v2, v3, v4, v5, v6, v7)
    y, x, c = (lax.axis_index(a) for a in ROW)
    me = (y * SIDE[1] + x) * SIDE[2] + c

    def place(dy, dx, dc):
        return (y + dy) & (SIDE[0] - 1), (x + dx) & (SIDE[1] - 1), (c + dc) & (SIDE[2] - 1)

    def device(p):
        return dict(zip(ROW, p, strict=True))

    def far_first(t):
        half = (t + 1) >> 1
        return 4 + half - 2 * half * (t & 1)

    def for_peers(act):
        def turn_of(k, _):
            for i in range(8):
                dy = (4, 3, 5, 2, 6, 1, 7, 0)[i]
                dx = far_first((k + i) & 7)
                for dc in range(2):
                    if i == 7 and dc == 0:
                        pl.when(k != 0)(functools.partial(act, place(dy, dx, dc)))
                    else:
                        act(place(dy, dx, dc))
            return 0

        lax.fori_loop(0, 8, turn_of, 0)

    barrier = pltpu.get_barrier_semaphore()

    def greet(p):
        pl.semaphore_signal(barrier, inc=1, device_id=device(p), device_id_type=MESH)

    for_peers(greet)
    loads = [
        pltpu.make_async_copy(h, v, table_sem.at[i])
        for i, (h, v) in enumerate(zip(hbm_tables, vmem_tables, strict=True))
    ]
    for load in loads:
        load.start()

    def start_exchange(src, dst, n, phase):
        rows = src.shape[1] // PEERS

        def send(p):
            to = (p[0] * SIDE[1] + p[1]) * SIDE[2] + p[2]
            pltpu.make_async_remote_copy(
                src_ref=src.at[n, pl.ds(pl.multiple_of(to * rows, rows), rows)],
                dst_ref=dst.at[n, pl.ds(pl.multiple_of(me * rows, rows), rows)],
                send_sem=send_sem.at[n, phase],
                recv_sem=take_sem.at[n, phase],
                device_id=device(p),
                device_id_type=MESH,
            ).start()

        for_peers(send)
        own = pl.ds(pl.multiple_of(me * rows, rows), rows)
        dst[n, own, :] = src[n, own, :]

    def whole(src, dst, n, phase):
        rows = src.shape[1] // PEERS
        return pltpu.make_async_remote_copy(
            src_ref=src.at[n, pl.ds(0, rows * (PEERS - 1))],
            dst_ref=dst.at[n, pl.ds(0, rows * (PEERS - 1))],
            send_sem=send_sem.at[n, phase],
            recv_sem=take_sem.at[n, phase],
            device_id=device((y, x, c)),
            device_id_type=MESH,
        )

    def pack_rows(fields, dst, n):
        shares = 16 // len(fields) // each
        wide = width // shares
        for j in range(wide // LANES):
            block = [
                f[:, s * wide + j * LANES : s * wide + (j + 1) * LANES] for f in fields for s in range(shares)
            ]
            dst[n, j * LANES : (j + 1) * LANES, :] = jnp.concatenate(block, axis=0).T

    def unpack_rows(src, n, count):
        shares = 16 // count // each
        wide = width // shares
        rows = each * rows_local
        got = [src[n, j * LANES : (j + 1) * LANES, :].T for j in range(wide // LANES)]
        return [
            jnp.concatenate(
                [g[(f * shares + s) * rows : (f * shares + s + 1) * rows] for s in range(shares) for g in got], axis=1
            )
            for f in range(count)
        ]

    def unpack_columns(src, n, count):
        deep = src.shape[1] // PEERS
        for s in range(deep):
            turn[s * LANES : (s + 1) * LANES, :] = src[n, pl.ds(s, PEERS, stride=deep), :].T
        out = [[] for _ in range(count)]
        for a in range(rows_local):
            got = turn[pl.ds(a, deep * 16, stride=rows_local), :].reshape(deep, count, 16 // count, LANES)
            for f in range(count):
                out[f].append(got[:, f].reshape(deep * 16 // count, LANES))
        return [jnp.concatenate(o, axis=1) for o in out]

    def pack_columns(fields, dst, n):
        count = len(fields)
        deep = dst.shape[1] // PEERS
        for a in range(rows_local):
            got = [f[:, a * LANES : (a + 1) * LANES].reshape(deep, 1, 16 // count, LANES) for f in fields]
            turn[pl.ds(a, deep * 16, stride=rows_local), :] = jnp.concatenate(got, axis=1).reshape(deep * 16, LANES)
        for s in range(deep):
            dst[n, pl.ds(s, PEERS, stride=deep), :] = turn[s * LANES : (s + 1) * LANES, :].T

    def per_plane(shape, plane_of_row, first_plane):
        out = jnp.zeros(shape, jnp.float32)
        for p in range(each):
            out = jnp.where(plane_of_row == p, mobility_ref[first_plane + p], out)
        return out

    def ready(i):
        loads[i].wait()
        return vmem_tables[i]

    waited = set()

    def table(i):
        if i not in waited:
            waited.add(i)
            loads[i].wait()
        return vmem_tables[i]

    def start_rows(n):
        field = x_ref[n * each : (n + 1) * each].reshape(each * rows_local, width)
        local = field * field * field - field + stiffness * product(field, by_row(table(0)))
        held[n] = local
        pack_rows([field, local], send1, n)

    def columns_middle(n):
        field, local = unpack_columns(take1, n, 2)
        potential = local + stiffness * product(field, by_column(table(1)))
        slope = product(potential, by_column(table(2)))
        rows = lax.broadcasted_iota(jnp.int32, (field.shape[0], LANES), 0)
        scale = per_plane(rows.shape, rows % each, n * each)
        scale = jnp.concatenate([scale] * (field.shape[1] // LANES), axis=1)
        weight = scale / (1.0 + field * field)
        pack_columns([potential, product(weight * slope, by_column(table(2)))], send2, n)

    def rows_middle(n):
        potential, spread = unpack_rows(take2, n, 2)
        slope = product(potential, by_row(table(3)))
        field = x_ref[n * each : (n + 1) * each].reshape(each * rows_local, width)
        rows = lax.broadcasted_iota(jnp.int32, (field.shape[0], LANES), 0)
        scale = per_plane(rows.shape, rows // rows_local, n * each)
        scale = jnp.concatenate([scale] * (width // LANES), axis=1)
        weight = scale / (1.0 + field * field)
        total = spread + product(weight * slope, by_row(table(3)))
        first, last = total[:, : width // 2], total[:, width // 2 :]
        basis = table(4)
        spectrum = jnp.concatenate(
            [product(first + last, dense_half(basis, 0)), product(first - last, dense_half(basis, 1))], axis=1
        )
        pack_rows([spectrum], send3, n)

    def columns_solve(n):
        deep = take3.shape[1] // PEERS
        shares = 16 // each
        rows = lax.broadcasted_iota(jnp.int32, (deep * 16, LANES), 0)
        slot_y = (rows % 16) // each * (width // shares) + me * deep + rows // 16
        scale = per_plane(rows.shape, rows % each, n * each)
        step = 2.0 * math.pi / width
        wave_y = slots(slot_y, width)[0].astype(jnp.float32) * step
        length = PEERS * rows_local
        slot_x = lax.broadcasted_iota(jnp.int32, (8, length), 1)
        wave_x = slots(slot_x, length)[0].astype(jnp.float32) * (2.0 * math.pi / length)
        square_x = (wave_x * wave_x)[:1]
        wide = length // LANES
        square = jnp.concatenate([wave_y * wave_y] * wide, axis=1) + square_x
        denom = 1.0 + time_step * jnp.concatenate([scale] * wide, axis=1) * (
            stabilizer * square + stiffness * square * square
        )
        factor = time_step / denom
        whole(send3, take3, n, 2).wait_recv()
        (spectrum,) = unpack_columns(take3, n, 1)
        solved = product(spectrum, dense(table(5))) * factor
        pack_columns([product(solved, dense(table(6)))], send4, n)

    def residual():
        total = jnp.sum(sum_all[...], axis=0)
        length = PEERS * rows_local
        mean = jnp.sum(total, axis=1, keepdims=True) * (1.0 / (length * width))
        row = lax.broadcasted_iota(jnp.int32, (planes, LANES), 0)
        target = jnp.zeros((planes, LANES), jnp.float32)
        for p in range(planes):
            target = jnp.where(row == p, target_ref[p], target)
        residual_ref[...] = mean - target

    def rows_end(n):
        (spectrum,) = unpack_rows(take4, n, 1)
        back = table(7)
        even = product(spectrum[:, : width // 2], dense_half(back, 0))
        odd = product(spectrum[:, width // 2 :], dense_half(back, 1))
        change = jnp.concatenate([even + odd, even - odd], axis=1).reshape(each, rows_local, width)
        shift = residual_ref[n * each : (n + 1) * each, :][:, None, :]
        shift = jnp.concatenate([shift] * (width // LANES), axis=2)
        out_ref[n * each : (n + 1) * each] = x_ref[n * each : (n + 1) * each] + change - shift

    def sum_slot(stage, p):
        return p[0] if stage else p[1] * SIDE[2] + p[2]

    def sum_copy(stage, index, p, sender):
        src, dst = ((sum_mine, sum_row), (sum_total, sum_all))[stage]
        slot = sum_slot(stage, sender)
        return pltpu.make_async_remote_copy(
            src_ref=src, dst_ref=dst.at[slot], send_sem=sum_send.at[stage, index], recv_sem=sum_take.at[stage, slot],
            device_id=device(p), device_id_type=MESH,
        )

    def start_sums(stage, places):
        for i, d in enumerate(places):
            sum_copy(stage, i, place(*d), (y, x, c)).start()
        src, dst = ((sum_mine, sum_row), (sum_total, sum_all))[stage]
        dst[sum_slot(stage, (y, x, c))] = src[...]

    def take_sums(stage, places):
        for i, d in enumerate(places):
            sum_copy(stage, i, (y, x, c), place(*d)).wait_recv()

    near = [(0, dx, dc) for dx in range(SIDE[1]) for dc in range(SIDE[2])][1:]
    across = [(dy, 0, 0) for dy in range(1, SIDE[0])]

    for n in range(ncs):
        start_rows(n)
    summed = jnp.sum(x_ref[...], axis=1)
    part = summed[:, :LANES]
    for j in range(1, width // LANES):
        part = part + summed[:, j * LANES : (j + 1) * LANES]
    sum_mine[...] = part

    pl.semaphore_wait(barrier, PEERS - 1)
    for n in range(ncs):
        start_exchange(send1, take1, n, 0)
    start_sums(0, near)
    for n in range(ncs):
        whole(send1, take1, n, 0).wait_recv()
        columns_middle(n)
        start_exchange(send2, take2, n, 1)
    take_sums(0, near)
    sum_total[...] = jnp.sum(sum_row[...], axis=0)
    start_sums(1, across)
    for n in range(ncs):
        whole(send2, take2, n, 1).wait_recv()
        rows_middle(n)
        start_exchange(send3, take3, n, 2)
    take_sums(1, across)
    residual()
    for n in range(ncs):
        columns_solve(n)
        start_exchange(send4, take4, n, 3)
    for n in range(ncs):
        whole(send4, take4, n, 3).wait_recv()
        rows_end(n)
    for n in range(ncs):
        for phase, (src, dst) in enumerate(((send1, take1), (send2, take2), (send3, take3), (send4, take4))):
            whole(src, dst, n, phase).wait_send()
    for stage, places in enumerate((near, across)):
        for i, d in enumerate(places):
            sum_copy(stage, i, place(*d), (y, x, c)).wait_send()


def local(concentration, target_mass, mobility):
    planes, rows_local, width = concentration.shape
    data = tables(width, rows_local)
    ncs = CHUNKS
    two = pltpu.VMEM((ncs, PEERS * planes // ncs, LANES), jnp.float32)
    one = pltpu.VMEM((ncs, PEERS * planes // ncs // 2, LANES), jnp.float32)
    vmem = pl.BlockSpec(memory_space=pltpu.VMEM)
    smem = pl.BlockSpec(memory_space=pltpu.SMEM)
    updated, residual = pl.pallas_call(
        kernel,
        out_shape=(
            jax.ShapeDtypeStruct(concentration.shape, jnp.float32),
            jax.ShapeDtypeStruct((planes, LANES), jnp.float32),
        ),
        in_specs=[vmem, smem, smem] + [pl.BlockSpec(memory_space=pl.ANY)] * len(data),
        out_specs=(vmem, vmem),
        scratch_shapes=[pltpu.VMEM(t.shape, jnp.bfloat16) for t in data]
        + [two] * 4
        + [one] * 4
        + [
            pltpu.VMEM((PEERS * planes // ncs, LANES), jnp.float32),
            pltpu.VMEM((ncs, planes // ncs * rows_local, width), jnp.float32),
            pltpu.VMEM((planes, LANES), jnp.float32),
            pltpu.VMEM((SIDE[1] * SIDE[2], planes, LANES), jnp.float32),
            pltpu.VMEM((planes, LANES), jnp.float32),
            pltpu.VMEM((SIDE[0], planes, LANES), jnp.float32),
            pltpu.SemaphoreType.DMA((len(data),)),
            pltpu.SemaphoreType.DMA((ncs, 4)),
            pltpu.SemaphoreType.DMA((ncs, 4)),
            pltpu.SemaphoreType.DMA((2, SIDE[1] * SIDE[2])),
            pltpu.SemaphoreType.DMA((2, SIDE[1] * SIDE[2])),
        ],
        compiler_params=pltpu.CompilerParams(
            collective_id=0, has_side_effects=True, vmem_limit_bytes=60 * 2**20
        ),
    )(concentration, target_mass, mobility, *[jnp.asarray(t) for t in data])
    return updated, residual[:, 0]


def solution(mesh):
    torus = Mesh(mesh.devices.reshape(mesh.shape["grp"], *SIDE), ("grp", *ROW))
    in_specs = (P("grp", ROW, None), P("grp"), P("grp"))
    out_specs = (P("grp", ROW, None), P("grp"))
    return jax.shard_map(local, mesh=torus, in_specs=in_specs, out_specs=out_specs, check_vma=False)
```

time: 418 us -> 94.5 us (0.23); the launches traced: 410 us -> 94.3 us
  local copies, waits for them, and re-layouts: 139 us -> 2.97 us
  starting transfers between devices: 97.4 us -> 0 us
  Pallas kernels: 0 us -> 90.7 us
  matrix products: 65.4 us -> 0 us
  waiting for transfers between devices: 50.5 us -> 0 us
  blocking collectives: 38.8 us -> 0 us
  other arithmetic: 17.4 us -> 0 us
    all_to_all x8 -> x0, starting transfers between devices: 97.4 us -> none  [the longest x1 28.1 us: local(): lax.all_to_all(half_real, ROW, split_axis=1, concat_axis=2, tiled=True)]
    pallas_call x0 -> x1, Pallas kernels: none -> 90.7 us  [local(): pl.pallas_call(kernel, out_shape=(jax.ShapeDtypeStruct(concentration.shap...]
    dot_general x56 -> x0, matrix products: 65.4 us -> none  [contract(): return jnp.einsum(pattern, operand, table, precision=lax.Precision.HIGHEST)]
    unnamed x24 -> x1, local copies, waits for them, and re-layouts: 58.3 us -> 1.67 us
    all_to_all x8 -> x0, waiting for transfers between devices: 50.5 us -> none  [the longest x1 11.1 us: local(): lax.all_to_all(back_real, ROW, split_axis=1, concat_axis=2, tiled=True)]
    reshape x15 -> x0, local copies, waits for them, and re-layouts: 42.9 us -> none  [the longest x2 6.34 us: forward_cols(): imag_part.reshape(shape)]
    psum x3 -> x0, blocking collectives: 38.8 us -> none  [by_axis(): x = lax.psum(x, axis)]
    all_to_all x9 -> x0, local copies, waits for them, and re-layouts: 36.3 us -> none  [the longest x1 6.59 us: local(): lax.all_to_all(change_real, ROW, split_axis=1, concat_axis=2, tiled=True)]
  transfers between devices with their start and end apart: 8 -> 0, of which waited for: 6 -> 0; matrix products, arithmetic and copies ran while one was open for 24% -> 0% of each run, Pallas kernels for 0% -> 0%
where the time goes in v1:
time: 94.5 us; the launch traced here: 94.3 us
  Pallas kernels  90.7 us (96%)
  local copies, waits for them, and re-layouts  2.97 us (3%)
    pallas_call x1, Pallas kernels, local(): pl.pallas_call(kernel, out_shape=(jax.ShapeDtypeStruct(concentration.shap...  90.7 us

profile of v1, /device:TPU:513, one launch (start us, length us, event | category | flops | bytes accessed | tf_op | source)
XLA Modules:
  0.0 94.3 jit_solution(14768525944712268270)
XLA Ops:
  0.6 90.7 %shard_map.122 = (f32[8,8,1024]{2,1,0:T(8,128)}, f32[8,128]{1,0:T(8,128)}) custom-call(f32[8,8,1024]{2,1,0:T(8,128)} %x_ref.1, f32[8]{0:T(128)} %target_ref.1, f32[8]{0:T(128)} %mobility_ref.1, bf16[2,4,256,256]{3,2,1,0:T(8,128)(2,1)} %constant.16.clone.t0, bf16[2,7,256,256]{3,2,1,0:T(8,128)(2,1)} %constant.17.clone.t1, ...), custom_call_target="tpu_custom_call" | custom-call | tf_op jit(solution)/shard_map/pallas_call | solution.py:431
  91.4 1.3 %slice_reduce_fusion = f32[8]{0:T(128)} fusion(f32[8,128]{1,0:T(8,128)} %get-tuple-element.5), kind=kLoop, calls=%fused_computation | loop fusion | bytes 64 | tf_op jit(solution)/shard_map/slice | solution.py:459
  92.7 1.7 %copy.14 = f32[8,8,1024]{2,1,0:T(8,128)} copy(f32[8,8,1024]{2,1,0:T(8,128)} %get-tuple-element.8) | data formatting | bytes 524288

commit v2 on v1

v2 whole, which is shorter than its diff:
```python
import functools
import math

import jax
import jax.numpy as jnp
import ml_dtypes
import numpy as np
from jax import lax
from jax.experimental import pallas as pl
from jax.experimental.pallas import tpu as pltpu
from jax.sharding import Mesh
from jax.sharding import PartitionSpec as P

ROW = ("row_0", "row_1", "row_2")
MESH = pl.DeviceIdType.MESH
SIDE = (8, 8, 2)
CHIPS = SIDE[0] * SIDE[1]
CORES = SIDE[2]
LANES = 128
CHUNKS = 2

stiffness = 1.0
time_step = 0.05
stabilizer = 2.0


def split(table):
    high = table.astype(ml_dtypes.bfloat16)
    low = (table - high.astype(np.float64)).astype(ml_dtypes.bfloat16)
    return np.stack([high, low])


def circulants(length):
    position = np.arange(length)
    signed = np.where(position < length // 2, position, position - length)
    angular = signed * (2.0 * math.pi / length)
    derivative = np.where(position == length // 2, 0.0, angular)
    offset = (position[None, :] - position[:, None]) % length
    second = np.fft.ifft(angular**2).real[offset]
    first = np.fft.ifft(1j * derivative).real[offset]
    return second, first


def real_basis(length):
    wave, is_sine = slots(np.arange(length), length)
    angle = np.outer(np.arange(length), wave) % length * (2.0 * math.pi / length)
    plain = (wave == 0) | (wave == length // 2)
    scale = np.where(plain, np.sqrt(1.0 / length), np.sqrt(2.0 / length))
    return np.where(is_sine & ~plain, np.sin(angle), np.cos(angle)) * scale


def slots(slot, length):
    quarter = length // 4
    odd = slot // (2 * quarter)
    within = slot % (2 * quarter)
    is_sine = within // quarter
    wave = 2 * (within % quarter) + odd
    nyquist = (is_sine == 1) & (wave == 0)
    if isinstance(slot, np.ndarray):
        return np.where(nyquist, length // 2, wave), is_sine == 1
    return jnp.where(nyquist, length // 2, wave), is_sine == 1


def halves(matrix, order):
    half = matrix.shape[0] // 2
    near, far = matrix[order][:, order], matrix[order][:, order + half]
    return np.stack([near + far, near - far]) / 2


@functools.cache
def tables(length):
    second, first = circulants(length)
    basis = real_basis(length)
    half = length // 2
    rows = np.arange(half)
    columns = rows.reshape(CHIPS // 2, CORES, -1).transpose(2, 1, 0).reshape(-1)
    row_basis, column_basis = (np.stack([basis[o][:, :half], basis[o][:, half:]]) for o in (rows, columns))
    return tuple(
        split(t)
        for t in (
            halves(second, rows),
            halves(second, columns),
            halves(first, columns),
            halves(first, rows),
            row_basis,
            column_basis,
            np.swapaxes(column_basis, 1, 2),
            np.swapaxes(row_basis, 1, 2),
        )
    )


def parts(x):
    high = x.astype(jnp.bfloat16)
    low = (x - high.astype(jnp.float32)).astype(jnp.bfloat16)
    return high, jnp.concatenate([high, low], axis=0)


def product(x, pieces):
    m = x.shape[0]
    high, both = parts(x)
    inputs, outputs, piece = pieces
    out = []
    for j in range(outputs):
        total = None
        for i in range(inputs):
            at = slice(i * 256, (i + 1) * 256)
            wide = jnp.dot(both[:, at], piece(i, j, 0), preferred_element_type=jnp.float32)
            narrow = jnp.dot(high[:, at], piece(i, j, 1), preferred_element_type=jnp.float32)
            term = (wide, narrow)
            total = term if total is None else (total[0] + wide, total[1] + narrow)
        out.append(total[0][:m] + total[0][m:] + total[1])
    return jnp.concatenate(out, axis=1)


def table_pieces(ref, which):
    n = ref.shape[2] // 256
    return n, n, lambda i, j, part: ref[part, which, i * 256 : (i + 1) * 256, j * 256 : (j + 1) * 256]


def analyse(x, ref):
    return product(x[0] + x[1], table_pieces(ref, 0)), product(x[0] - x[1], table_pieces(ref, 1))


def synthesise(z, ref):
    even, odd = product(z[0], table_pieces(ref, 0)), product(z[1], table_pieces(ref, 1))
    return even + odd, even - odd


def circulant(x, ref):
    even, odd = analyse(x, ref)
    return even + odd, even - odd


def cut(x):
    half = x.shape[1] // 2
    return x[:, :half], x[:, half:]


def join(x):
    return jnp.concatenate(x, axis=1)


def kernel(
    x_ref, target_hbm, mobility_hbm,
    t0, t1, t2, t3, t4, t5, t6, t7,
    out_ref, residual_ref,
    v0, v1, v2, v3, v4, v5, v6, v7,
    send1, take1, send2, take2, send3, take3, send4, take4,
    turn, mine, local_part, rows_of,
    sum0, sum1, take_sum0, take_sum1, target_ref, mobility_ref,
    load_sem, send_sem, take_sem, swap_send, swap_take, sum_send, sum_take,
):
    planes, rows_local, width = x_ref.shape
    ncs = CHUNKS
    own = planes // CORES
    each = own // ncs
    vmem_tables = (v0, v1, v2, v3, v4, v5, v6, v7)
    y, x, c = (lax.axis_index(a) for a in ROW)
    chip = y * SIDE[1] + x
    other = 1 - c

    def device(p):
        return dict(zip(ROW, p, strict=True))

    def far_first(t):
        half = (t + 1) >> 1
        return 4 + half - 2 * half * (t & 1)

    def for_chips(act):
        def turn_of(k, _):
            for i in range(8):
                to_y = (y + (4, 3, 5, 2, 6, 1, 7, 0)[i]) & (SIDE[0] - 1)
                to_x = (x + far_first((k + i) & 7)) & (SIDE[1] - 1)
                if i == 7:
                    pl.when(k != 0)(functools.partial(act, to_y, to_x))
                else:
                    act(to_y, to_x)
            return 0

        lax.fori_loop(0, 8, turn_of, 0)

    first_loads = [
        pltpu.make_async_copy(a, b, load_sem.at[i])
        for i, (a, b) in enumerate(((x_ref, mine), (mobility_hbm, mobility_ref), (target_hbm, target_ref)))
    ]
    loads = [
        pltpu.make_async_copy(h, v, load_sem.at[3 + i])
        for i, (h, v) in enumerate(zip((t0, t1, t2, t3, t4, t5, t6, t7), vmem_tables, strict=True))
    ]
    for load in (first_loads[0], loads[0], *first_loads[1:]):
        load.start()

    barrier = pltpu.get_barrier_semaphore()

    def greet(to_y, to_x):
        for core in range(CORES):
            pl.semaphore_signal(barrier, inc=1, device_id=device((to_y, to_x, core)), device_id_type=MESH)

    for_chips(greet)
    pl.semaphore_signal(barrier, inc=1, device_id=device((y, x, other)), device_id_type=MESH)
    for load in loads[1:]:
        load.start()

    def spot(core, position, deep):
        return pl.ds(pl.multiple_of((core * CHIPS + position) * deep, deep), deep)

    def copy_out(src_ref, dst_ref, n, phase, p):
        return pltpu.make_async_remote_copy(
            src_ref=src_ref, dst_ref=dst_ref, send_sem=send_sem.at[n, phase], recv_sem=take_sem.at[n, phase],
            device_id=device(p), device_id_type=MESH,
        )

    def start_to_cores(src, dst, n, phase):
        deep = src.shape[1] // CHIPS // CORES
        here = spot(c, chip, deep)

        def send_one(to_y, to_x, core):
            there = spot(core, to_y * SIDE[1] + to_x, deep)
            copy_out(src.at[n, there], dst.at[n, here], n, phase, (to_y, to_x, core)).start()

        def send(to_y, to_x):
            for core in range(CORES):
                send_one(to_y, to_x, core)

        for_chips(send)
        send_one(y, x, other)
        dst[n, here, :] = src[n, here, :]

    def start_to_chips(src, dst, n, phase):
        deep = src.shape[2] // CHIPS
        here = spot(0, chip, deep)

        def send(to_y, to_x):
            there = spot(0, to_y * SIDE[1] + to_x, deep)
            copy_out(src.at[n, :, there], dst.at[n, :, here], n, phase, (to_y, to_x, c)).start()

        for_chips(send)
        for core in range(CORES):
            dst[n, core, here, :] = src[n, core, here, :]

    def whole(src, dst, n, phase):
        if len(src.shape) == 3:
            deep = src.shape[1] // CHIPS // CORES
            at = (n, pl.ds(0, deep * (CHIPS * CORES - 1)))
        else:
            deep = src.shape[2] // CHIPS
            at = (n, slice(None), pl.ds(0, deep * (CHIPS - 1)))
        return copy_out(src.at[at], dst.at[at], n, phase, (y, x, other))

    def part(ref, n, core):
        if len(ref.shape) == 3:
            rows = ref.shape[1] // CORES
            return ref.at[n, pl.ds(core * rows, rows)], rows // CHIPS
        return ref.at[n, core], ref.shape[2] // CHIPS

    def swap(n):
        return pltpu.make_async_remote_copy(
            src_ref=mine.at[pl.ds(other * own + n * each, each)],
            dst_ref=rows_of.at[n, c],
            send_sem=swap_send.at[n],
            recv_sem=swap_take.at[n],
            device_id=device((y, x, other)),
            device_id_type=MESH,
        )

    def pack_rows(fields, dst, n, core):
        dst, _ = part(dst, n, core)
        shares = 16 // len(fields) // each
        wide = width // shares
        for j in range(wide // LANES):
            block = [
                f[:, s * wide + j * LANES : s * wide + (j + 1) * LANES] for f in fields for s in range(shares)
            ]
            dst[j * LANES : (j + 1) * LANES, :] = jnp.concatenate(block, axis=0).T

    def unpack_rows(src, n, count):
        shares = 16 // count // each
        wide = width // shares
        rows = each * rows_local
        out = [[] for _ in range(count)]
        for core in range(CORES):
            ref, _ = part(src, n, core)
            got = [ref[j * LANES : (j + 1) * LANES, :].T for j in range(wide // LANES)]
            for f in range(count):
                pieces = [g[(f * shares + s) * rows : (f * shares + s + 1) * rows] for s in range(shares) for g in got]
                out[f].append(jnp.concatenate(pieces, axis=1))
        return [jnp.concatenate(o, axis=0) for o in out]

    some = CHIPS // 2

    def low_half(rows):
        return lax.broadcasted_iota(jnp.int32, (rows, LANES), 1) < LANES // 2

    def unpack_columns(src, n, count):
        refs = [part(src, n, core) for core in range(CORES)]
        deep = refs[0][1]
        for s in range(deep):
            got = [
                ref[pl.ds(s + hi * some * deep, some, stride=deep), :] for hi in range(2) for ref, _ in refs
            ]
            turn[s * LANES : (s + 1) * LANES, :] = jnp.concatenate(got, axis=0).T
        out = [([], []) for _ in range(count)]
        low = low_half(deep * 16 // count)
        for a in range(0, rows_local, 2):
            pair = [
                turn[pl.ds(a + i, deep * 16, stride=rows_local), :].reshape(deep, count, 16 // count, LANES)
                for i in range(2)
            ]
            for f in range(count):
                one, two = (g[:, f].reshape(deep * 16 // count, LANES) for g in pair)
                out[f][0].append(jnp.where(low, one, pltpu.roll(two, LANES // 2, 1)))
                out[f][1].append(jnp.where(low, pltpu.roll(one, LANES // 2, 1), two))
        return [tuple(jnp.concatenate(h, axis=1) for h in o) for o in out]

    def pack_columns(fields, dst, n):
        count = len(fields)
        refs = [part(dst, n, core) for core in range(CORES)]
        deep = refs[0][1]
        low = low_half(deep * 16 // count)
        for a in range(0, rows_local, 2):
            at = slice(a // 2 * LANES, (a // 2 + 1) * LANES)
            pair = ([], [])
            for f in fields:
                near, far = f[0][:, at], f[1][:, at]
                pair[0].append(jnp.where(low, near, pltpu.roll(far, LANES // 2, 1)))
                pair[1].append(jnp.where(low, pltpu.roll(near, LANES // 2, 1), far))
            for i in range(2):
                got = [g.reshape(deep, 1, 16 // count, LANES) for g in pair[i]]
                turn[pl.ds(a + i, deep * 16, stride=rows_local), :] = jnp.concatenate(got, axis=1).reshape(
                    deep * 16, LANES
                )
        for s in range(deep):
            both = turn[s * LANES : (s + 1) * LANES, :].T
            for hi in range(2):
                for core, (ref, _) in enumerate(refs):
                    at = (hi * CORES + core) * some
                    ref[pl.ds(s + hi * some * deep, some, stride=deep), :] = both[at : at + some]

    def per_plane(shape, plane_of_row, n):
        out = jnp.zeros(shape, jnp.float32)
        for p in range(each):
            out = jnp.where(plane_of_row == p, mobility_ref[c * own + n * each + p], out)
        return out

    waited = set()

    def table(i):
        if i not in waited:
            waited.add(i)
            loads[i].wait()
        return vmem_tables[i]

    def start_fields():
        first_loads[0].wait()
        field = mine[...].reshape(planes * rows_local, width)
        local = field * field * field - field + stiffness * join(circulant(cut(field), table(0)))
        local_part[...] = local.reshape(planes, rows_local, width)
        for n in range(ncs):
            for core in range(CORES):
                at = slice(core * own + n * each, core * own + (n + 1) * each)
                fields = [ref[at].reshape(each * rows_local, width) for ref in (mine, local_part)]
                pack_rows(fields, send1, n, core)

    def columns_middle(n):
        field, local = unpack_columns(take1, n, 2)
        potential = [u + stiffness * v for u, v in zip(local, circulant(field, table(1)), strict=True)]
        slope = circulant(potential, table(2))
        rows = lax.broadcasted_iota(jnp.int32, (field[0].shape[0], LANES), 0)
        scale = per_plane(rows.shape, rows % each, n)
        scale = jnp.concatenate([scale] * (field[0].shape[1] // LANES), axis=1)
        flux = [scale / (1.0 + f * f) * g for f, g in zip(field, slope, strict=True)]
        pack_columns([potential, circulant(flux, table(2))], send2, n)

    def row_weight(n):
        for p in range(each):
            rows_of[n, c, p] = mine[c * own + n * each + p]
        swap(n).wait_recv()
        field = rows_of[n].reshape(CORES * each * rows_local, width)
        rows = lax.broadcasted_iota(jnp.int32, (field.shape[0], LANES), 0)
        scale = per_plane(rows.shape, rows // rows_local % each, n)
        scale = jnp.concatenate([scale] * (width // LANES), axis=1)
        rows_of[n] = (scale / (1.0 + field * field)).reshape(rows_of.shape[1:])

    def rows_middle(n):
        potential, spread = unpack_rows(take2, n, 2)
        slope = join(circulant(cut(potential), table(3)))
        weight = rows_of[n].reshape(slope.shape)
        total = spread + join(circulant(cut(weight * slope), table(3)))
        spectrum = join(analyse(cut(total), table(4)))
        rows = each * rows_local
        for core in range(CORES):
            pack_rows([spectrum[core * rows : (core + 1) * rows]], send3, n, core)

    def columns_solve(n):
        deep = take3.shape[2] // CHIPS
        shares = 16 // each
        rows = lax.broadcasted_iota(jnp.int32, (deep * 16, LANES), 0)
        slot_y = rows % 16 // each * (width // shares) + chip * deep + rows // 16
        scale = per_plane(rows.shape, rows % each, n)
        step = 2.0 * math.pi / width
        wave_y = slots(slot_y, width)[0].astype(jnp.float32) * step
        length = CHIPS * CORES * rows_local
        slot_x = lax.broadcasted_iota(jnp.int32, (8, length), 1)
        wave_x = slots(slot_x, length)[0].astype(jnp.float32) * (2.0 * math.pi / length)
        square_x = (wave_x * wave_x)[:1]
        wide = length // LANES
        square = jnp.concatenate([wave_y * wave_y] * wide, axis=1) + square_x
        denom = 1.0 + time_step * jnp.concatenate([scale] * wide, axis=1) * (
            stabilizer * square + stiffness * square * square
        )
        factor = time_step / denom
        whole(send3, take3, n, 2).wait_recv()
        (spectrum,) = unpack_columns(take3, n, 1)
        solved = [z * f for z, f in zip(analyse(spectrum, table(5)), cut(factor), strict=True)]
        pack_columns([synthesise(solved, table(6))], send4, n)

    def residual():
        total = jnp.sum(take_sum1[...], axis=0)
        length = CHIPS * CORES * rows_local
        mean = jnp.sum(total, axis=1, keepdims=True) * (1.0 / (length * width))
        row = lax.broadcasted_iota(jnp.int32, (planes, LANES), 0)
        first_loads[2].wait()
        target = jnp.zeros((planes, LANES), jnp.float32)
        for p in range(planes):
            target = jnp.where(row == p, target_ref[p], target)
        residual_ref[...] = mean - target

    def rows_end(n):
        (spectrum,) = unpack_rows(take4, n, 1)
        change = join(synthesise(cut(spectrum), table(7))).reshape(CORES, each, rows_local, width)
        for core in range(CORES):
            at = slice(core * own + n * each, core * own + (n + 1) * each)
            down = jnp.concatenate([residual_ref[at][:, None, :]] * (width // LANES), axis=2)
            out_ref[at] = mine[at] + change[core] - down

    sums = ((sum0, take_sum0), (sum1, take_sum1))
    near = [(0, dx, dc) for dx in range(SIDE[1]) for dc in range(SIDE[2])][1:]
    across = [(dy, 0, 0) for dy in range(1, SIDE[0])]

    def place(dy, dx, dc):
        return (y + dy) & (SIDE[0] - 1), (x + dx) & (SIDE[1] - 1), (c + dc) & (SIDE[2] - 1)

    def sum_slot(stage, p):
        return p[0] if stage else p[1] * SIDE[2] + p[2]

    def sum_copy(stage, index, p, sender):
        src, dst = sums[stage]
        slot = sum_slot(stage, sender)
        return pltpu.make_async_remote_copy(
            src_ref=src, dst_ref=dst.at[slot], send_sem=sum_send.at[stage, index], recv_sem=sum_take.at[stage, slot],
            device_id=device(p), device_id_type=MESH,
        )

    def start_sums(stage, places):
        for i, d in enumerate(places):
            sum_copy(stage, i, place(*d), (y, x, c)).start()
        src, dst = sums[stage]
        dst[sum_slot(stage, (y, x, c))] = src[...]

    def take_sums(stage, places):
        for i, d in enumerate(places):
            sum_copy(stage, i, (y, x, other), place(*d)).wait_recv()

    start_fields()
    summed = jnp.sum(mine[...], axis=1)
    partial = summed[:, :LANES]
    for j in range(1, width // LANES):
        partial = partial + summed[:, j * LANES : (j + 1) * LANES]
    sum0[...] = partial

    pl.semaphore_wait(barrier, CHIPS * CORES - 1)
    for n in range(ncs):
        start_to_cores(send1, take1, n, 0)
    start_sums(0, near)
    for n in range(ncs):
        swap(n).start()
    first_loads[1].wait()
    for n in range(ncs):
        row_weight(n)
    for n in range(ncs):
        whole(send1, take1, n, 0).wait_recv()
        columns_middle(n)
        start_to_chips(send2, take2, n, 1)
    take_sums(0, near)
    sum1[...] = jnp.sum(take_sum0[...], axis=0)
    start_sums(1, across)
    for n in range(ncs):
        whole(send2, take2, n, 1).wait_recv()
        rows_middle(n)
        start_to_chips(send3, take3, n, 2)
    for n in range(ncs):
        columns_solve(n)
        start_to_cores(send4, take4, n, 3)
    take_sums(1, across)
    residual()
    for n in range(ncs):
        whole(send4, take4, n, 3).wait_recv()
        rows_end(n)
    for n in range(ncs):
        for phase, (src, dst) in enumerate(((send1, take1), (send2, take2), (send3, take3), (send4, take4))):
            whole(src, dst, n, phase).wait_send()
        swap(n).wait_send()
    for stage, places in enumerate((near, across)):
        for i, d in enumerate(places):
            sum_copy(stage, i, place(*d), (y, x, c)).wait_send()


def hand_over(updated_ref, residual_ref, out_ref, out_residual_ref):
    out_ref[...] = updated_ref[...]
    for p in range(out_residual_ref.shape[0]):
        out_residual_ref[p] = residual_ref[p, 0]


def local(concentration, target_mass, mobility):
    planes, rows_local, width = concentration.shape
    data = tables(width)
    ncs = CHUNKS
    each = planes // CORES // ncs
    rows = CHIPS * CORES * each
    shape = {1: (ncs, 2 * rows, LANES), 2: (ncs, CORES, rows, LANES), 3: (ncs, CORES, rows // 2, LANES), 4: (ncs, rows, LANES)}
    vmem = pl.BlockSpec(memory_space=pltpu.VMEM)
    updated, residual = pl.pallas_call(
        kernel,
        out_shape=(
            jax.ShapeDtypeStruct(concentration.shape, jnp.float32),
            jax.ShapeDtypeStruct((planes, LANES), jnp.float32),
        ),
        in_specs=[pl.BlockSpec(memory_space=pl.ANY)] * (3 + len(data)),
        out_specs=(vmem, vmem),
        scratch_shapes=[pltpu.VMEM(t.shape, jnp.bfloat16) for t in data]
        + [pltpu.VMEM(shape[phase], jnp.float32) for phase in (1, 2, 3, 4) for _ in range(2)]
        + [
            pltpu.VMEM((2 * rows, LANES), jnp.float32),
            pltpu.VMEM((planes, rows_local, width), jnp.float32),
            pltpu.VMEM((planes, rows_local, width), jnp.float32),
            pltpu.VMEM((ncs, CORES, each, rows_local, width), jnp.float32),
            pltpu.VMEM((planes, LANES), jnp.float32),
            pltpu.VMEM((planes, LANES), jnp.float32),
            pltpu.VMEM((SIDE[1] * SIDE[2], planes, LANES), jnp.float32),
            pltpu.VMEM((SIDE[0], planes, LANES), jnp.float32),
            pltpu.SMEM((planes,), jnp.float32),
            pltpu.SMEM((planes,), jnp.float32),
            pltpu.SemaphoreType.DMA((3 + len(data),)),
            pltpu.SemaphoreType.DMA((ncs, 4)),
            pltpu.SemaphoreType.DMA((ncs, 4)),
            pltpu.SemaphoreType.DMA((ncs,)),
            pltpu.SemaphoreType.DMA((ncs,)),
            pltpu.SemaphoreType.DMA((2, SIDE[1] * SIDE[2])),
            pltpu.SemaphoreType.DMA((2, SIDE[1] * SIDE[2])),
        ],
        compiler_params=pltpu.CompilerParams(
            collective_id=0, has_side_effects=True, vmem_limit_bytes=30 * 2**20
        ),
    )(concentration, target_mass, mobility, *[jnp.asarray(t) for t in data])
    smem = pl.BlockSpec(memory_space=pltpu.SMEM)
    return pl.pallas_call(
        hand_over,
        out_shape=(
            jax.ShapeDtypeStruct(concentration.shape, jnp.float32),
            jax.ShapeDtypeStruct((planes,), jnp.float32),
        ),
        in_specs=[vmem, smem],
        out_specs=(vmem, smem),
    )(updated, residual)


def solution(mesh):
    torus = Mesh(mesh.devices.reshape(mesh.shape["grp"], *SIDE), ("grp", *ROW))
    in_specs = (P("grp", ROW, None), P("grp"), P("grp"))
    out_specs = (P("grp", ROW, None), P("grp"))
    return jax.shard_map(local, mesh=torus, in_specs=in_specs, out_specs=out_specs, check_vma=False)
```

time: 94.5 us -> 97 us (1.026)
  local copies, waits for them, and re-layouts: 2.97 us -> 16.3 us
  Pallas kernels: 90.7 us -> 79.6 us
    unnamed x1 -> x26, local copies, waits for them, and re-layouts: 1.67 us -> 16.3 us
    pallas_call x1, Pallas kernels: 90.7 us -> 77.9 us  [local(): pl.pallas_call(kernel, out_shape=(jax.ShapeDtypeStruct(concentration.shap...]
    pallas_call x0 -> x1, Pallas kernels: none -> 1.69 us  [local(): pl.pallas_call(hand_over, out_shape=(jax.ShapeDtypeStruct(concentration.s...]
    slice x1 -> x0, local copies, waits for them, and re-layouts: 1.3 us -> none  [local(): return (updated, residual[:, 0])]
where the time goes in v2:
time: 97 us; the launch traced here: 96.5 us
  Pallas kernels  79.6 us (82%)
  local copies, waits for them, and re-layouts  16.3 us (17%)
    pallas_call x1, Pallas kernels, local(): pl.pallas_call(kernel, out_shape=(jax.ShapeDtypeStruct(concentration.shap...  77.9 us
    unnamed x26, local copies, waits for them, and re-layouts  16.3 us

profile of v2, /device:TPU:513, one launch (start us, length us, event | category | flops | bytes accessed | tf_op | source)
XLA Modules:
  0.0 96.5 jit_solution(12916393097640768377)
XLA Ops:
  0.6 0.0 copy-start
  0.6 1.6 %copy-done = bf16[2,2,512,512]{3,2,1,0:T(8,128)(2,1)S(1)} copy-done((bf16[2,2,512,512]{3,2,1,0:T(8,128)(2,1)S(1)}, bf16[2,2,512,512]{3,2,1,0:T(8,128)(2,1)}, u32[]{:S(2)}) %copy-start) | copy-done | bytes 2097176
  2.2 0.0 copy-start.1
  2.2 1.6 %copy-done.1 = bf16[2,2,512,512]{3,2,1,0:T(8,128)(2,1)S(1)} copy-done((bf16[2,2,512,512]{3,2,1,0:T(8,128)(2,1)S(1)}, bf16[2,2,512,512]{3,2,1,0:T(8,128)(2,1)}, u32[]{:S(2)}) %copy-start.1) | copy-done | bytes 2097176
  3.8 0.0 copy-start.2
  3.8 1.6 %copy-done.2 = bf16[2,2,512,512]{3,2,1,0:T(8,128)(2,1)S(1)} copy-done((bf16[2,2,512,512]{3,2,1,0:T(8,128)(2,1)S(1)}, bf16[2,2,512,512]{3,2,1,0:T(8,128)(2,1)}, u32[]{:S(2)}) %copy-start.2) | copy-done | bytes 2097176
  5.4 0.0 copy-start.3
  5.4 1.6 %copy-done.3 = bf16[2,2,512,512]{3,2,1,0:T(8,128)(2,1)S(1)} copy-done((bf16[2,2,512,512]{3,2,1,0:T(8,128)(2,1)S(1)}, bf16[2,2,512,512]{3,2,1,0:T(8,128)(2,1)}, u32[]{:S(2)}) %copy-start.3) | copy-done | bytes 2097176
  7.0 0.0 copy-start.4
  7.0 1.6 %copy-done.4 = bf16[2,2,512,512]{3,2,1,0:T(8,128)(2,1)S(1)} copy-done((bf16[2,2,512,512]{3,2,1,0:T(8,128)(2,1)S(1)}, bf16[2,2,512,512]{3,2,1,0:T(8,128)(2,1)}, u32[]{:S(2)}) %copy-start.4) | copy-done | bytes 2097176
  8.6 0.0 copy-start.5
  8.6 1.6 %copy-done.5 = bf16[2,2,512,512]{3,2,1,0:T(8,128)(2,1)S(1)} copy-done((bf16[2,2,512,512]{3,2,1,0:T(8,128)(2,1)S(1)}, bf16[2,2,512,512]{3,2,1,0:T(8,128)(2,1)}, u32[]{:S(2)}) %copy-start.5) | copy-done | bytes 2097176
  10.2 0.0 copy-start.6
  10.2 1.6 %copy-done.6 = bf16[2,2,512,512]{3,2,1,0:T(8,128)(2,1)S(1)} copy-done((bf16[2,2,512,512]{3,2,1,0:T(8,128)(2,1)S(1)}, bf16[2,2,512,512]{3,2,1,0:T(8,128)(2,1)}, u32[]{:S(2)}) %copy-start.6) | copy-done | bytes 2097176
  11.8 0.0 copy-start.7
  11.8 1.6 %copy-done.7 = bf16[2,2,512,512]{3,2,1,0:T(8,128)(2,1)S(1)} copy-done((bf16[2,2,512,512]{3,2,1,0:T(8,128)(2,1)S(1)}, bf16[2,2,512,512]{3,2,1,0:T(8,128)(2,1)}, u32[]{:S(2)}) %copy-start.7) | copy-done | bytes 2097176
  13.4 0.0 copy-start.8
  13.4 0.9 copy-done.8
  14.3 0.0 copy-start.11
  14.3 0.7 copy-done.11
  15.0 0.0 copy-start.12
  15.0 0.7 copy-done.12
  15.6 77.9 %shard_map.122 = (f32[8,8,1024]{2,1,0:T(8,128)S(1)}, f32[8,128]{1,0:T(8,128)S(1)}) custom-call(f32[8,8,1024]{2,1,0:T(8,128)S(1)} %copy-done.8, f32[8]{0:T(128)S(1)} %copy-done.11, f32[8]{0:T(128)S(1)} %copy-done.12, bf16[2,2,512,512]{3,2,1,0:T(8,128)(2,1)S(1)} %copy-done.7, bf16[2,2,512,512]{3,2,1,0:T(8,128)(2,1)S(1)} %copy-done.6, ...), custom_call_target="tpu_custom_call" | custom-call | tf_op jit(solution)/shard_map/pallas_call | solution.py:523
  93.6 0.0 copy-start.9
  93.6 0.7 copy-done.9
  94.3 0.0 copy-start.10
  94.3 0.6 copy-done.10
  94.9 1.7 %shard_map.123 = (f32[8,8,1024]{2,1,0:T(8,128)}, f32[8]{0:T(128)}) custom-call(f32[8,8,1024]{2,1,0:T(8,128)} %copy-done.9, f32[8,128]{1,0:T(8,128)} %copy-done.10), custom_call_target="tpu_custom_call" | custom-call | tf_op jit(solution)/shard_map/pallas_call | solution.py:557
Async XLA Ops:
  0.6 1.6 %copy-start = (bf16[2,2,512,512]{3,2,1,0:T(8,128)(2,1)S(1)}, bf16[2,2,512,512]{3,2,1,0:T(8,128)(2,1)}, u32[]{:S(2)}) copy-start(bf16[2,2,512,512]{3,2,1,0:T(8,128)(2,1)} %constant.23.clone.t7) | copy-start | bytes 6291460
  2.2 1.6 %copy-start.1 = (bf16[2,2,512,512]{3,2,1,0:T(8,128)(2,1)S(1)}, bf16[2,2,512,512]{3,2,1,0:T(8,128)(2,1)}, u32[]{:S(2)}) copy-start(bf16[2,2,512,512]{3,2,1,0:T(8,128)(2,1)} %constant.22.clone.t6) | copy-start | bytes 6291460
  3.8 1.6 %copy-start.2 = (bf16[2,2,512,512]{3,2,1,0:T(8,128)(2,1)S(1)}, bf16[2,2,512,512]{3,2,1,0:T(8,128)(2,1)}, u32[]{:S(2)}) copy-start(bf16[2,2,512,512]{3,2,1,0:T(8,128)(2,1)} %constant.21.clone.t5) | copy-start | bytes 6291460
  5.4 1.6 %copy-start.3 = (bf16[2,2,512,512]{3,2,1,0:T(8,128)(2,1)S(1)}, bf16[2,2,512,512]{3,2,1,0:T(8,128)(2,1)}, u32[]{:S(2)}) copy-start(bf16[2,2,512,512]{3,2,1,0:T(8,128)(2,1)} %constant.20.clone.t4) | copy-start | bytes 6291460
  7.0 1.6 %copy-start.4 = (bf16[2,2,512,512]{3,2,1,0:T(8,128)(2,1)S(1)}, bf16[2,2,512,512]{3,2,1,0:T(8,128)(2,1)}, u32[]{:S(2)}) copy-start(bf16[2,2,512,512]{3,2,1,0:T(8,128)(2,1)} %constant.19.clone.t3) | copy-start | bytes 6291460
  8.6 1.6 %copy-start.5 = (bf16[2,2,512,512]{3,2,1,0:T(8,128)(2,1)S(1)}, bf16[2,2,512,512]{3,2,1,0:T(8,128)(2,1)}, u32[]{:S(2)}) copy-start(bf16[2,2,512,512]{3,2,1,0:T(8,128)(2,1)} %constant.18.clone.t2) | copy-start | bytes 6291460
  10.2 1.6 %copy-start.6 = (bf16[2,2,512,512]{3,2,1,0:T(8,128)(2,1)S(1)}, bf16[2,2,512,512]{3,2,1,0:T(8,128)(2,1)}, u32[]{:S(2)}) copy-start(bf16[2,2,512,512]{3,2,1,0:T(8,128)(2,1)} %constant.17.clone.t1) | copy-start | bytes 6291460
  11.8 1.6 %copy-start.7 = (bf16[2,2,512,512]{3,2,1,0:T(8,128)(2,1)S(1)}, bf16[2,2,512,512]{3,2,1,0:T(8,128)(2,1)}, u32[]{:S(2)}) copy-start(bf16[2,2,512,512]{3,2,1,0:T(8,128)(2,1)} %constant.16.clone.t0) | copy-start | bytes 6291460
  13.4 0.9 copy-start.8
  14.3 0.7 copy-start.11
  15.0 0.7 copy-start.12
  93.6 0.7 copy-start.9
  94.3 0.6 copy-start.10

commit v3 on v2

--- a/solution.py
+++ b/solution.py
@@ -268,11 +268,10 @@
         dst, _ = part(dst, n, core)
         shares = 16 // len(fields) // each
         wide = width // shares
-        for j in range(wide // LANES):
-            block = [
-                f[:, s * wide + j * LANES : s * wide + (j + 1) * LANES] for f in fields for s in range(shares)
-            ]
-            dst[j * LANES : (j + 1) * LANES, :] = jnp.concatenate(block, axis=0).T
+        some = min(wide, LANES)
+        for j in range(0, wide, some):
+            block = [f[:, s * wide + j : s * wide + j + some] for f in fields for s in range(shares)]
+            dst[j : j + some, :] = jnp.concatenate(block, axis=0).T
 
     def unpack_rows(src, n, count):
         shares = 16 // count // each
@@ -281,7 +280,8 @@
         out = [[] for _ in range(count)]
         for core in range(CORES):
             ref, _ = part(src, n, core)
-            got = [ref[j * LANES : (j + 1) * LANES, :].T for j in range(wide // LANES)]
+            some = min(wide, LANES)
+            got = [ref[j : j + some, :].T for j in range(0, wide, some)]
             for f in range(count):
                 pieces = [g[(f * shares + s) * rows : (f * shares + s + 1) * rows] for s in range(shares) for g in got]
                 out[f].append(jnp.concatenate(pieces, axis=1))
@@ -550,7 +550,7 @@
             pltpu.SemaphoreType.DMA((2, SIDE[1] * SIDE[2])),
         ],
         compiler_params=pltpu.CompilerParams(
-            collective_id=0, has_side_effects=True, vmem_limit_bytes=30 * 2**20
+            collective_id=0, has_side_effects=True, vmem_limit_bytes=60 * 2**20
         ),
     )(concentration, target_mass, mobility, *[jnp.asarray(t) for t in data])
     smem = pl.BlockSpec(memory_space=pltpu.SMEM)

time: 97 us -> 81 us (0.84)
  local copies, waits for them, and re-layouts: 16.3 us -> 0 us
    unnamed x26 -> x0, local copies, waits for them, and re-layouts: 16.3 us -> none
where the time goes in v3:
time: 81 us; the launch traced here: 80.8 us
  Pallas kernels  80.2 us (99%)
    pallas_call x1, Pallas kernels, local(): pl.pallas_call(kernel, out_shape=(jax.ShapeDtypeStruct(concentration.shap...  78.5 us
    pallas_call x1, Pallas kernels, local(): pl.pallas_call(hand_over, out_shape=(jax.ShapeDtypeStruct(concentration.s...  1.69 us

profile of v3, /device:TPU:513, one launch (start us, length us, event | category | flops | bytes accessed | tf_op | source)
XLA Modules:
  0.0 80.8 jit_solution(9230145554139424350)
XLA Ops:
  0.6 78.5 %shard_map.122 = (f32[8,8,1024]{2,1,0:T(8,128)}, f32[8,128]{1,0:T(8,128)}) custom-call(f32[8,8,1024]{2,1,0:T(8,128)} %x_ref.1, f32[8]{0:T(128)} %target_hbm.1, f32[8]{0:T(128)} %mobility_hbm.1, bf16[2,2,512,512]{3,2,1,0:T(8,128)(2,1)} %constant.16.clone.t0, bf16[2,2,512,512]{3,2,1,0:T(8,128)(2,1)} %constant.17.clone.t1, ...), custom_call_target="tpu_custom_call" | custom-call | tf_op jit(solution)/shard_map/pallas_call | solution.py:523
  79.1 1.7 %shard_map.123 = (f32[8,8,1024]{2,1,0:T(8,128)}, f32[8]{0:T(128)}) custom-call(f32[8,8,1024]{2,1,0:T(8,128)} %get-tuple-element.4.updated_ref, f32[8,128]{1,0:T(8,128)} %get-tuple-element.5.residual_ref), custom_call_target="tpu_custom_call" | custom-call | tf_op jit(solution)/shard_map/pallas_call | solution.py:557

commit v4 on v3

--- a/solution.py
+++ b/solution.py
@@ -141,6 +141,22 @@
     return jnp.concatenate(x, axis=1)
 
 
+def far_first():
+    groups = {}
+    for dy in range(SIDE[0]):
+        for dx in range(SIDE[1]):
+            far = min(dy, SIDE[0] - dy) + min(dx, SIDE[1] - dx)
+            way = (2 * dy > SIDE[0], 2 * dx > SIDE[1])
+            if far:
+                groups.setdefault(far, {}).setdefault(way, []).append((dy, dx))
+    out = []
+    for far in sorted(groups, reverse=True):
+        ways = [groups[far][w] for w in ((0, 0), (1, 1), (0, 1), (1, 0)) if w in groups[far]]
+        for turn in range(max(map(len, ways))):
+            out += [w[turn] for w in ways if turn < len(w)]
+    return out
+
+
 def kernel(
     x_ref, target_hbm, mobility_hbm,
     t0, t1, t2, t3, t4, t5, t6, t7,
@@ -163,22 +179,9 @@
     def device(p):
         return dict(zip(ROW, p, strict=True))
 
-    def far_first(t):
-        half = (t + 1) >> 1
-        return 4 + half - 2 * half * (t & 1)
-
     def for_chips(act):
-        def turn_of(k, _):
-            for i in range(8):
-                to_y = (y + (4, 3, 5, 2, 6, 1, 7, 0)[i]) & (SIDE[0] - 1)
-                to_x = (x + far_first((k + i) & 7)) & (SIDE[1] - 1)
-                if i == 7:
-                    pl.when(k != 0)(functools.partial(act, to_y, to_x))
-                else:
-                    act(to_y, to_x)
-            return 0
-
-        lax.fori_loop(0, 8, turn_of, 0)
+        for dy, dx in far_first():
+            act((y + dy) & (SIDE[0] - 1), (x + dx) & (SIDE[1] - 1))
 
     first_loads = [
         pltpu.make_async_copy(a, b, load_sem.at[i])
@@ -386,8 +389,16 @@
         potential, spread = unpack_rows(take2, n, 2)
         slope = join(circulant(cut(potential), table(3)))
         weight = rows_of[n].reshape(slope.shape)
-        total = spread + join(circulant(cut(weight * slope), table(3)))
-        spectrum = join(analyse(cut(total), table(4)))
+        both = jnp.concatenate([weight * slope, spread], axis=0)
+        count = slope.shape[0]
+        quarter = width // 4
+        place_of = lax.broadcasted_iota(jnp.int32, (8, quarter), 1)[:1]
+        spectrum = []
+        for odd, z in enumerate(analyse(cut(both), table(4))):
+            wave = (2 * place_of + odd).astype(jnp.float32) * (2.0 * math.pi / width)
+            cosine, sine = z[:count, :quarter], z[:count, quarter:]
+            spectrum += [z[count:, :quarter] + wave * sine, z[count:, quarter:] - wave * cosine]
+        spectrum = join(spectrum)
         rows = each * rows_local
         for core in range(CORES):
             pack_rows([spectrum[core * rows : (core + 1) * rows]], send3, n, core)

time: 81 us -> 77.9 us (0.962)
  Pallas kernels: 80.2 us -> 77 us
    pallas_call x1, Pallas kernels: 78.5 us -> 75.3 us  [local(): pl.pallas_call(kernel, out_shape=(jax.ShapeDtypeStruct(concentration.shap...]
where the time goes in v4:
time: 77.9 us; the launch traced here: 77.8 us
  Pallas kernels  77 us (99%)
  between operations  0.8 us (1%)
    pallas_call x1, Pallas kernels, local(): pl.pallas_call(kernel, out_shape=(jax.ShapeDtypeStruct(concentration.shap...  75.3 us
    pallas_call x1, Pallas kernels, local(): pl.pallas_call(hand_over, out_shape=(jax.ShapeDtypeStruct(concentration.s...  1.69 us

profile of v4, /device:TPU:513, one launch (start us, length us, event | category | flops | bytes accessed | tf_op | source)
XLA Modules:
  0.0 77.8 jit_solution(17469918637822488474)
XLA Ops:
  0.6 75.3 %shard_map.122 = (f32[8,8,1024]{2,1,0:T(8,128)}, f32[8,128]{1,0:T(8,128)}) custom-call(f32[8,8,1024]{2,1,0:T(8,128)} %x_ref.1, f32[8]{0:T(128)} %target_hbm.1, f32[8]{0:T(128)} %mobility_hbm.1, bf16[2,2,512,512]{3,2,1,0:T(8,128)(2,1)} %constant.16.clone.t0, bf16[2,2,512,512]{3,2,1,0:T(8,128)(2,1)} %constant.17.clone.t1, ...), custom_call_target="tpu_custom_call" | custom-call | tf_op jit(solution)/shard_map/pallas_call | solution.py:534
  75.9 1.7 %shard_map.123 = (f32[8,8,1024]{2,1,0:T(8,128)}, f32[8]{0:T(128)}) custom-call(f32[8,8,1024]{2,1,0:T(8,128)} %get-tuple-element.4.updated_ref, f32[8,128]{1,0:T(8,128)} %get-tuple-element.5.residual_ref), custom_call_target="tpu_custom_call" | custom-call | tf_op jit(solution)/shard_map/pallas_call | solution.py:568
